TPU v7x, 32 devices: a whole 2x2x4 slice. The times are simulated.
32 devices in a mesh: seq: 8 (over z, core), fsdp: 4 (over y, x).
Axes of the slice: x: 2, y: 2, z: 4, core: 2. Of those that a mesh axis runs over, the one named last changes fastest.
Arguments:
- patches: bfloat16 [4, 1024, 3072], P('fsdp', 'seq'), may hold values from -6 to 6
- weight_codes: int32 [3072, 3072], P('fsdp'), may hold values from -448 to 448
- block_scales: float32 [24, 24], P('fsdp'), may hold values from 2.5e-05 to 0.0001
- key_proj: bfloat16 [4, 1024, 3072], P('fsdp', 'seq'), may hold values from -6 to 6
- value_proj: bfloat16 [4, 1024, 3072], P('fsdp', 'seq'), may hold values from -6 to 6
- query_gain: float32 [3072], replicated, may hold values from 1 to 10
- key_gain: float32 [3072], replicated, may hold values from 1 to 10
Outputs:
- attended: bfloat16 [4, 1024, 3072], P('fsdp', 'seq')
All inputs are finite; a program needn't handle non-finite values.
Results may differ from a plain program's by a relative error of at most 0.007.
The roundings to bfloat16 on the way count: a program that leaves them out, or rounds other values in their place, can miss the bound.
Values may be sent and summed in bfloat16 or wider, within the bound.
A program may use at most 192 MiB of HBM per device.

v0:
```python
import functools
import math
import jax
import jax.numpy as jnp
from jax import lax
from jax.experimental import pallas as pl
from jax.experimental.pallas import tpu as pltpu
from jax.sharding import PartitionSpec as P

HEADS = 48
HDIM = 64
BLOCK = 128


NORM_FLOOR = 0.25


def head_norm(projected, gain_row):
    shaped = projected.reshape(projected.shape[:-1] + (HEADS, HDIM))
    average = jnp.mean(shaped, axis=-1, keepdims=True)
    centred = shaped - average
    spread = jnp.mean(centred * centred, axis=-1, keepdims=True)
    normed = centred * lax.rsqrt(spread + NORM_FLOOR) * gain_row.reshape(HEADS, HDIM)
    return normed.astype(jnp.bfloat16)


def dequantize(weight_codes, block_scales):
    row_count, column_count = weight_codes.shape
    blocked = weight_codes.astype(jnp.float32).reshape(
        row_count // BLOCK, BLOCK, column_count // BLOCK, BLOCK
    )
    return (
        (blocked * block_scales[:, None, :, None])
        .reshape(row_count, column_count)
        .astype(jnp.bfloat16)
    )


def start_of(query_view):
    image_count, token_count, head_count = (
        query_view.shape[0],
        query_view.shape[1],
        query_view.shape[2],
    )
    return (
        jnp.full((image_count, token_count, head_count), -1e30, jnp.float32),
        jnp.zeros((image_count, token_count, head_count), jnp.float32),
        jnp.zeros(query_view.shape, jnp.float32),
    )


def attend_block(query_view, state_now, key_view, value_view):
    running_max, running_sum, weighted = state_now
    scores = jnp.einsum(
        "ithd,ishd->iths", query_view, key_view, preferred_element_type=jnp.float32
    ) * HDIM ** (-0.5)
    newest = jnp.maximum(running_max, jnp.max(scores, axis=-1))
    probability = jnp.exp(scores - newest[..., None])
    running_sum = jnp.sum(probability, axis=-1)
    blended = jnp.einsum(
        "iths,ishd->ithd",
        probability.astype(jnp.bfloat16),
        value_view,
        preferred_element_type=jnp.float32,
    )
    weighted = blended
    return (newest, running_sum, weighted)


def per_device(patches, weight_codes, block_scales, key_proj, value_proj, query_gain, key_gain):
    image_count, token_count, feature_count = patches.shape
    flat_rows = patches.reshape(image_count * token_count, feature_count)
    key_norm = head_norm(key_proj.astype(jnp.float32), key_gain)
    value_view = value_proj.reshape(image_count, token_count, HEADS, HDIM)
    local_weight = dequantize(weight_codes, block_scales)
    group_rows = lax.all_to_all(flat_rows, "fsdp", split_axis=1, concat_axis=0, tiled=True)
    queries = lax.psum_scatter(
        jnp.dot(group_rows, local_weight, preferred_element_type=jnp.float32),
        "fsdp",
        scatter_dimension=0,
        tiled=True,
    )
    query_view = head_norm(queries, query_gain).reshape(image_count, token_count, HEADS, HDIM)
    finished = attend_block(
        query_view,
        start_of(query_view),
        lax.all_gather(key_norm, "seq", axis=1, tiled=True),
        lax.all_gather(value_view, "seq", axis=1, tiled=True),
    )
    attended = finished[2] / finished[1][..., None]
    return attended.reshape(image_count, token_count, HEADS * HDIM).astype(jnp.bfloat16)


MESH = pl.DeviceIdType.MESH
LANES = 128
CORES = 2
GRID = 2


def column_norm(values, gain_row):
    lane = lambda axis: lax.broadcasted_iota(jnp.int32, (LANES, LANES), axis) < HDIM
    spread_out = jnp.where(lane(0) == lane(1), 1.0 / HDIM, 0.0).astype(jnp.bfloat16)
    spread_out = jnp.concatenate([spread_out, spread_out], axis=0)

    def mean_of(t):
        high = t.astype(jnp.bfloat16)
        low = (t - high.astype(jnp.float32)).astype(jnp.bfloat16)
        return jnp.dot(jnp.concatenate([high, low], axis=1), spread_out, preferred_element_type=jnp.float32)

    centred = values - mean_of(values)
    normed = centred * lax.rsqrt(mean_of(centred * centred) + NORM_FLOOR) * gain_row
    return normed.astype(jnp.bfloat16)


def fused_kernel(
    n, fn, patches, codes, scales, key, value, query_gain, key_gain, out,
    pbuf, cbuf, wbuf, kraw, vbuf, knorm, qsend, qbuf, obuf,
    local_sem, code_sem, p_send, p_recv, fw_send, fw_recv, w_send, w_recv,
    kv_send, kv_recv, q_send, q_recv, o_send, o_recv, own_sem,
):
    s, f = lax.axis_index("seq"), lax.axis_index("fsdp")
    m = n // 2
    half, place = s // m, lax.rem(s, m)
    tokens = patches.shape[0]
    rows, columns = codes.shape
    width = columns // n
    chunks = width // LANES
    group = m * tokens
    chips = m // CORES
    partner = s + 1 - 2 * lax.rem(s, CORES)

    def chip_mate(d):
        return half * m + lax.rem(place + d * CORES, m)

    def rows_of(device):
        return pl.ds(pl.multiple_of(lax.rem(device, m) * tokens, tokens), tokens)

    def all_rows_of(device):
        return pl.ds(pl.multiple_of(device * tokens, tokens), tokens)

    def owned(device):
        return pl.multiple_of((lax.rem(device, m) * 2 + device // m) * width, LANES)

    def chunk_column(q):
        side = jnp.where(q < chunks, 1 - half, half)
        return pl.multiple_of((place * 2 + side) * width + lax.rem(q, chunks) * LANES, LANES)

    code_copies = []
    for q in range(2 * chunks):
        code_copies.append(pltpu.make_async_copy(
            codes.at[:, pl.ds(chunk_column(q), LANES)], cbuf.at[q], code_sem.at[q]))
        code_copies[-1].start()
    own_copies = [
        pltpu.make_async_copy(patches, pbuf.at[rows_of(s)], local_sem.at[0]),
        pltpu.make_async_copy(key.at[:, pl.ds(owned(s), width)], kraw.at[all_rows_of(s)], local_sem.at[1]),
        pltpu.make_async_copy(value.at[:, pl.ds(owned(s), width)], vbuf.at[all_rows_of(s)], local_sem.at[2]),
    ]
    for copy in own_copies:
        copy.start()

    barrier = pltpu.get_barrier_semaphore()
    for d in range(1, n):
        pl.semaphore_signal(barrier, inc=1, device_id={"seq": lax.rem(s + d, n)}, device_id_type=MESH)
    for d in range(1, fn):
        pl.semaphore_signal(barrier, inc=1, device_id={"fsdp": lax.rem(f + d, fn)}, device_id_type=MESH)
    pl.semaphore_wait(barrier, n - 1 + fn - 1)

    def remote(src, dst, send, recv, **device):
        return pltpu.make_async_remote_copy(
            src_ref=src, dst_ref=dst, send_sem=send, recv_sem=recv, device_id=device, device_id_type=MESH)

    patch_copies = [remote(patches, pbuf.at[rows_of(s)], p_send.at[0], p_recv.at[0], seq=partner)]
    for d in range(1, chips):
        patch_copies.append(remote(patches, pbuf.at[rows_of(s)], p_send.at[d], p_recv.at[d], seq=chip_mate(d)))
    for copy in patch_copies[1:] + patch_copies[:1]:
        copy.start()

    far = place // CORES == jnp.where(half == 0, 0, chips - 1)

    def kv_copy(which, d):
        src, dst = ((key, kraw), (value, vbuf))[which]
        to = lax.rem(s + d, n)
        return remote(
            src.at[:, pl.ds(owned(to), width)], dst.at[all_rows_of(s)],
            kv_send.at[which, d], kv_recv.at[which, d], seq=to)

    def start_kv(behind_patches):
        for which in range(2):
            for step in range(1, n):
                d = jnp.where(half == 0, step, n - step)
                to = lax.rem(s + d, n)
                to_far = lax.rem(to, m) // CORES == jnp.where(to // m == 0, 0, chips - 1)
                over_pair = jnp.where(to // m == half, to // CORES != s // CORES, far & to_far)

                @pl.when(over_pair == behind_patches)
                def _():
                    kv_copy(which, d).start()

    start_kv(False)

    row_mate = f + 1 - 2 * lax.rem(f, GRID)
    column_mate = lax.rem(f + GRID, fn)

    def weight_copy(pair, way, start, size, to):
        at = pl.ds(pl.multiple_of(start, size), size)
        return remote(wbuf.at[pair, at], wbuf.at[pair, at], w_send.at[pair, way], w_recv.at[pair, way], fsdp=to)

    def near_copies(pair):
        return [
            weight_copy(pair, 0, f * rows, rows, row_mate),
            weight_copy(pair, 1, f * rows, rows, column_mate),
        ]

    def relay_copies(pair):
        part = rows // 2
        return [
            weight_copy(pair, 2, row_mate * rows, part, column_mate),
            weight_copy(pair, 3, column_mate * rows + part, part, row_mate),
        ]

    def relay(pair):
        for copy in near_copies(pair):
            copy.wait_recv()
        for copy in relay_copies(pair):
            copy.start()

    def relay_early():
        for pair in range(chunks - 1):
            relay(pair)
        for copy in near_copies(chunks - 1):
            copy.start()

    def dequantize_pair(pair, _):
        for side in range(2):
            q = 2 * pair + side
            pltpu.make_async_copy(
                codes.at[:, pl.ds(chunk_column(q), LANES)], cbuf.at[q], code_sem.at[q]).wait()
            for block in range(rows // BLOCK):
                scale = scales[block, chunk_column(q) // BLOCK]
                piece = cbuf[q, block * BLOCK:(block + 1) * BLOCK, :].astype(jnp.float32) * scale
                at = pl.ds(pl.multiple_of(f * rows + block * BLOCK, BLOCK), BLOCK)
                wbuf[pair, at, side * LANES:(side + 1) * LANES] = piece.astype(jnp.bfloat16)

        @pl.when(pair < chunks - 1)
        def _():
            for copy in near_copies(pair):
                copy.start()

        return 0

    lax.fori_loop(0, chunks, dequantize_pair, 0)

    own_copies[0].wait()

    def forward_copy(d):
        at = rows_of(half * m + lax.rem(place + m - d * CORES, m))
        return remote(pbuf.at[at], pbuf.at[at], fw_send.at[d], fw_recv.at[d], seq=partner)

    def patches_out():
        for copy in patch_copies[1:]:
            copy.wait_send()
        start_kv(True)

    def patches_in():
        for d in range(1, chips):
            patch_copies[d].wait_recv()
            forward_copy(d).start()

    @pl.when(far)
    def _():
        patches_out()
        relay_early()
        patches_in()

    @pl.when(jnp.logical_not(far))
    def _():
        patches_in()
        relay_early()

    patch_copies[0].wait()
    for d in range(1, chips):
        forward_copy(d).wait()

    other = lax.rem(s + m, n)
    half_rows = pl.ds(pl.multiple_of(half * group, group), group)

    def query_copy(k):
        return remote(qsend.at[k], qbuf.at[k, half_rows], q_send.at[k], q_recv.at[k], seq=other)

    def project(pair):
        for copy in near_copies(pair):
            copy.wait_send()
        for copy in relay_copies(pair):
            copy.wait()
        both = jnp.dot(pbuf[...], wbuf[pair], preferred_element_type=jnp.float32)
        for side in range(2):
            q = 2 * pair + side
            normed = column_norm(
                both[:, side * LANES:(side + 1) * LANES], query_gain[:, pl.ds(chunk_column(q), LANES)])
            if q < chunks:
                qsend[q] = normed
                query_copy(q).start()
            else:
                qbuf[q - chunks, half_rows] = normed

    early = (chunks + 2) // 2
    for pair in range(early):
        project(pair)
        if pair == 0:
            pl.when(jnp.logical_not(far))(patches_out)
    relay(chunks - 1)

    own_copies[1].wait()
    for d in range(1, n):
        kv_copy(0, d).wait()

    def key_chunk(k, _):
        at = pl.multiple_of(k * LANES, LANES)
        knorm[k] = column_norm(
            kraw[:, pl.ds(at, LANES)].astype(jnp.float32),
            key_gain[:, pl.ds(pl.multiple_of(owned(s) + at, LANES), LANES)])
        return 0

    lax.fori_loop(0, chunks, key_chunk, 0)

    own_copies[2].wait()
    for d in range(1, n):
        kv_copy(1, d).wait()

    tile = 2 * tokens
    exponent = HDIM ** (-0.5) * math.log2(math.e)

    def out_columns(k):
        return pl.ds(pl.multiple_of(owned(s) + k * LANES, LANES), LANES)

    def out_copy(k, to):
        d = lax.rem(to - s + n, n)
        return remote(obuf.at[k, all_rows_of(to)], out.at[:, out_columns(k)],
                      o_send.at[k, d], o_recv.at[k, d], seq=to)

    def own_out(k):
        return pltpu.make_async_copy(obuf.at[k, all_rows_of(s)], out.at[:, out_columns(k)], own_sem.at[k])

    first = lax.broadcasted_iota(jnp.int32, (tile, LANES), 1) < HDIM
    tiles = n // CORES

    def attend_step(step, _):
        k, i = step // tiles, lax.rem(step, tiles)
        own_side = half * chips + lax.rem(place // CORES + 1 + i, chips)
        chip = jnp.where(i < chips, (1 - half) * chips + i, own_side)
        here = pl.ds(pl.multiple_of(chip * tile, tile), tile)

        @pl.when(i == 0)
        def _():
            query_copy(k).wait()

        values = vbuf[:, pl.ds(pl.multiple_of(k * LANES, LANES), LANES)]
        keys = knorm[k]
        queries = qbuf[k, here]
        results = []
        for mine in (first, jnp.logical_not(first)):
            masked = jnp.where(mine, queries, jnp.zeros_like(queries))
            scores = lax.dot_general(
                masked, keys, (((1,), (1,)), ((), ())), preferred_element_type=jnp.float32)
            largest = jnp.max(scores, axis=-1, keepdims=True)
            probability = jnp.exp2((scores - largest) * exponent)
            normaliser = jnp.sum(probability, axis=-1, keepdims=True)
            blended = jnp.dot(
                probability.astype(jnp.bfloat16), values, preferred_element_type=jnp.float32)
            results.append(blended / normaliser)
        obuf[k, here] = jnp.where(first, results[0], results[1]).astype(jnp.bfloat16)
        for core in range(CORES):
            to = chip * CORES + core

            @pl.when(to != s)
            def _():
                out_copy(k, to).start()

            @pl.when(to == s)
            def _():
                own_out(k).start()

        return 0

    ready = 2 * early - chunks
    lax.fori_loop(0, ready * tiles, attend_step, 0)
    for pair in range(early, chunks):
        project(pair)
    lax.fori_loop(ready * tiles, chunks * tiles, attend_step, 0)

    def finish(k, _):
        own_out(k).wait()
        for d in range(1, n):
            out_copy(k, lax.rem(s + d, n)).wait()
        return 0

    lax.fori_loop(0, chunks, finish, 0)


def fused_per_device(n, fn, patches, weight_codes, block_scales, key_proj, value_proj, query_gain, key_gain):
    _, tokens, features = patches.shape
    rows, columns = weight_codes.shape
    width = columns // n
    chunks = width // LANES
    group = n // 2 * tokens
    bf16 = jnp.bfloat16
    dma = pltpu.SemaphoreType.DMA
    anywhere = pl.BlockSpec(memory_space=pl.ANY)
    vmem = pl.BlockSpec(memory_space=pltpu.VMEM)
    result = pl.pallas_call(
        functools.partial(fused_kernel, n, fn),
        out_shape=pltpu.VMEM((tokens, columns), bf16),
        in_specs=[anywhere, anywhere, pl.BlockSpec(memory_space=pltpu.SMEM), anywhere, anywhere, vmem, vmem],
        out_specs=vmem,
        scratch_shapes=[
            pltpu.VMEM((group, features), bf16),
            pltpu.VMEM((2 * chunks, rows, LANES), jnp.int32),
            pltpu.VMEM((chunks, features, 2 * LANES), bf16),
            pltpu.VMEM((n * tokens, width), bf16),
            pltpu.VMEM((n * tokens, width), bf16),
            pltpu.VMEM((chunks, n * tokens, LANES), bf16),
            pltpu.VMEM((chunks, group, LANES), bf16),
            pltpu.VMEM((chunks, n * tokens, LANES), bf16),
            pltpu.VMEM((chunks, n * tokens, LANES), bf16),
            dma((3,)), dma((2 * chunks,)),
            dma((n,)), dma((n,)), dma((n,)), dma((n,)),
            dma((chunks, fn)), dma((chunks, fn)),
            dma((2, n)), dma((2, n)),
            dma((chunks,)), dma((chunks,)),
            dma((chunks, n)), dma((chunks, n)), dma((chunks,)),
        ],
        compiler_params=pltpu.CompilerParams(
            collective_id=0, has_side_effects=True, vmem_limit_bytes=56 * 1024 * 1024),
    )(
        patches.reshape(tokens, features), weight_codes, block_scales,
        key_proj.reshape(tokens, columns), value_proj.reshape(tokens, columns),
        query_gain.reshape(1, columns), key_gain.reshape(1, columns),
    )
    return result.reshape(1, tokens, columns)


def solution(mesh):
    n, fn = mesh.shape["seq"], mesh.shape["fsdp"]
    specs = (
        P("fsdp", "seq", None), P("fsdp", None), P("fsdp", None),
        P("fsdp", "seq", None), P("fsdp", "seq", None), P(), P(),
    )

    def whole(*arrays):
        patches, weight_codes = arrays[:2]
        fits = patches.shape[0] == fn == GRID * GRID and weight_codes.shape[1] % (n * LANES) == 0 and n % (2 * CORES) == 0
        body = functools.partial(fused_per_device, n, fn) if fits else per_device
        return jax.shard_map(
            body, mesh=mesh, in_specs=specs, out_specs=P("fsdp", "seq", None), check_vma=False
        )(*arrays)

    return whole
```

profile of v0, /device:TPU:0, one launch (start us, length us, event | category | flops | bytes accessed | tf_op | source)
XLA Modules:
  0.0 77.6 jit_solution(307608278517055553)
XLA Ops:
  0.0 76.7 %shard_map.73 = bf16[128,3072]{1,0:T(8,128)(2,1)S(1)} custom-call(bf16[128,3072]{1,0:T(8,128)(2,1)} %bitcast.7, s32[768,3072]{1,0:T(8,128)} %codes.1, f32[6,24]{1,0:T(8,128)} %scales.1, bf16[128,3072]{1,0:T(8,128)(2,1)} %bitcast.8, bf16[128,3072]{1,0:T(8,128)(2,1)} %bitcast.9, f32[1,3072]{1,0:T(1,128)} %bitcast.10, f32[1,3072]{1,0:T(1,128)} %bitcast.11), custom_call_target="tpu_custom_call" | custom-call | tf_op jit(solution)/shard_map/pallas_call | solution.py:410
  76.7 0.9 %copy.9 = bf16[1,128,3072]{2,1,0:T(8,128)(2,1)} copy(bf16[1,128,3072]{2,1,0:T(8,128)(2,1)S(1)} %bitcast.6) | data formatting | bytes 1572864
where the time goes:
time: 77.8 us; the launch traced here: 77.6 us
  Pallas kernels  76.7 us (99%)
  local copies, waits for them, and re-layouts  0.88 us (1%)
    pallas_call x1, Pallas kernels, fused_per_device(): pl.pallas_call(functools.partial(fused_kernel, n, fn), out_shape=pltpu.VM...  76.7 us

commit v1 on v0

v1 whole, which is shorter than its diff:
```python
import functools
import math
import jax
import jax.numpy as jnp
from jax import lax
from jax.experimental import pallas as pl
from jax.experimental.pallas import tpu as pltpu
from jax.sharding import PartitionSpec as P

HEADS = 48
HDIM = 64
BLOCK = 128


NORM_FLOOR = 0.25


def head_norm(projected, gain_row):
    shaped = projected.reshape(projected.shape[:-1] + (HEADS, HDIM))
    average = jnp.mean(shaped, axis=-1, keepdims=True)
    centred = shaped - average
    spread = jnp.mean(centred * centred, axis=-1, keepdims=True)
    normed = centred * lax.rsqrt(spread + NORM_FLOOR) * gain_row.reshape(HEADS, HDIM)
    return normed.astype(jnp.bfloat16)


def dequantize(weight_codes, block_scales):
    row_count, column_count = weight_codes.shape
    blocked = weight_codes.astype(jnp.float32).reshape(
        row_count // BLOCK, BLOCK, column_count // BLOCK, BLOCK
    )
    return (
        (blocked * block_scales[:, None, :, None])
        .reshape(row_count, column_count)
        .astype(jnp.bfloat16)
    )


def start_of(query_view):
    image_count, token_count, head_count = (
        query_view.shape[0],
        query_view.shape[1],
        query_view.shape[2],
    )
    return (
        jnp.full((image_count, token_count, head_count), -1e30, jnp.float32),
        jnp.zeros((image_count, token_count, head_count), jnp.float32),
        jnp.zeros(query_view.shape, jnp.float32),
    )


def attend_block(query_view, state_now, key_view, value_view):
    running_max, running_sum, weighted = state_now
    scores = jnp.einsum(
        "ithd,ishd->iths", query_view, key_view, preferred_element_type=jnp.float32
    ) * HDIM ** (-0.5)
    newest = jnp.maximum(running_max, jnp.max(scores, axis=-1))
    probability = jnp.exp(scores - newest[..., None])
    running_sum = jnp.sum(probability, axis=-1)
    blended = jnp.einsum(
        "iths,ishd->ithd",
        probability.astype(jnp.bfloat16),
        value_view,
        preferred_element_type=jnp.float32,
    )
    weighted = blended
    return (newest, running_sum, weighted)


def per_device(patches, weight_codes, block_scales, key_proj, value_proj, query_gain, key_gain):
    image_count, token_count, feature_count = patches.shape
    flat_rows = patches.reshape(image_count * token_count, feature_count)
    key_norm = head_norm(key_proj.astype(jnp.float32), key_gain)
    value_view = value_proj.reshape(image_count, token_count, HEADS, HDIM)
    local_weight = dequantize(weight_codes, block_scales)
    group_rows = lax.all_to_all(flat_rows, "fsdp", split_axis=1, concat_axis=0, tiled=True)
    queries = lax.psum_scatter(
        jnp.dot(group_rows, local_weight, preferred_element_type=jnp.float32),
        "fsdp",
        scatter_dimension=0,
        tiled=True,
    )
    query_view = head_norm(queries, query_gain).reshape(image_count, token_count, HEADS, HDIM)
    finished = attend_block(
        query_view,
        start_of(query_view),
        lax.all_gather(key_norm, "seq", axis=1, tiled=True),
        lax.all_gather(value_view, "seq", axis=1, tiled=True),
    )
    attended = finished[2] / finished[1][..., None]
    return attended.reshape(image_count, token_count, HEADS * HDIM).astype(jnp.bfloat16)


MESH = pl.DeviceIdType.MESH
LANES = 128
CORES = 2
GRID = 2


def column_norm(values, gain_row):
    lane = lambda axis: lax.broadcasted_iota(jnp.int32, (LANES, LANES), axis) < HDIM
    spread_out = jnp.where(lane(0) == lane(1), 1.0 / HDIM, 0.0).astype(jnp.bfloat16)
    spread_out = jnp.concatenate([spread_out, spread_out], axis=0)

    def mean_of(t):
        high = t.astype(jnp.bfloat16)
        low = (t - high.astype(jnp.float32)).astype(jnp.bfloat16)
        return jnp.dot(jnp.concatenate([high, low], axis=1), spread_out, preferred_element_type=jnp.float32)

    centred = values - mean_of(values)
    normed = centred * lax.rsqrt(mean_of(centred * centred) + NORM_FLOOR) * gain_row
    return normed.astype(jnp.bfloat16)


def fused_kernel(
    n, fn, patches, codes, scales_in, key, value, query_gain_in, key_gain_in, out,
    pbuf, cbuf, wbuf, kv, qsend, qbuf, obuf, gains, scales,
    code_sem, scale_sem, gain_sem, mate_recv, rest_recv, p_send, near_recv, relay_recv, w_send,
    kv_send, kv_recv, q_send, q_recv, o_send, o_recv,
):
    s, f = lax.axis_index("seq"), lax.axis_index("fsdp")
    m = n // 2
    half, place = s // m, lax.rem(s, m)
    tokens = patches.shape[0]
    rows, columns = codes.shape
    width = columns // n
    chunks = width // LANES
    group = m * tokens
    chips = m // CORES
    core = lax.rem(s, CORES)
    partner = s + 1 - 2 * core

    barrier = pltpu.get_barrier_semaphore()
    for d in range(1, n):
        pl.semaphore_signal(barrier, inc=1, device_id={"seq": lax.rem(s + d, n)}, device_id_type=MESH)
    for d in range(1, fn):
        pl.semaphore_signal(barrier, inc=1, device_id={"fsdp": lax.rem(f + d, fn)}, device_id_type=MESH)

    def chip_mate(d):
        return half * m + lax.rem(place + d * CORES, m)

    def rows_of(device):
        return pl.ds(pl.multiple_of(lax.rem(device, m) * tokens, tokens), tokens)

    def all_rows_of(device):
        return pl.ds(pl.multiple_of(device * tokens, tokens), tokens)

    def owned(device):
        return pl.multiple_of((lax.rem(device, m) * 2 + device // m) * width, LANES)

    def owned_chunk(device, k):
        return pl.ds(pl.multiple_of(owned(device) + k * LANES, LANES), LANES)

    def chunk_column(q):
        side = jnp.where(q < chunks, 1 - half, half)
        return pl.multiple_of((place * 2 + side) * width + lax.rem(q, chunks) * LANES, LANES)

    def drain(ref, sem):
        pltpu.make_async_copy(ref, ref, sem).wait()

    pltpu.make_async_copy(scales_in, scales, scale_sem.at[0]).start()
    for q in range(2 * chunks):
        pltpu.make_async_copy(codes.at[:, pl.ds(chunk_column(q), LANES)], cbuf.at[q], code_sem.at[0]).start()
    pltpu.make_async_copy(patches, pbuf.at[rows_of(s)], rest_recv.at[0]).start()
    pltpu.make_async_copy(query_gain_in, gains.at[0], gain_sem.at[0]).start()
    pltpu.make_async_copy(key_gain_in, gains.at[1], gain_sem.at[0]).start()
    for k in range(chunks):
        for which, src in enumerate((key, value)):
            pltpu.make_async_copy(
                src.at[:, owned_chunk(s, k)], kv.at[k, which, all_rows_of(s)], kv_recv.at[k]).start()

    pl.semaphore_wait(barrier, n - 1 + fn - 1)

    def remote(src, dst, send, recv, **device):
        return pltpu.make_async_remote_copy(
            src_ref=src, dst_ref=dst, send_sem=send, recv_sem=recv, device_id=device, device_id_type=MESH)

    def mate_copy(d):
        return remote(patches, pbuf.at[rows_of(s)], p_send.at[0], mate_recv.at[d - 1], seq=chip_mate(d))

    for d in range(1, chips):
        mate_copy(d).start()

    far = place // CORES == jnp.where(half == 0, 0, chips - 1)

    def start_kv(to):
        def one(k, _):
            for which, src in enumerate((key, value)):
                remote(
                    src.at[:, owned_chunk(to, k)], kv.at[k, which, all_rows_of(s)],
                    kv_send.at[0], kv_recv.at[k], seq=to).start()
            return 0

        return one

    def kv_across():
        for j in range(chips):
            chip = jnp.where(half == 0, chips + j, chips - 1 - j)

            def both(k, _):
                for c in range(CORES):
                    start_kv(chip * CORES + c)(k, 0)
                return 0

            lax.fori_loop(0, chunks, both, 0)

    def kv_beside():
        for d in range(1, chips):
            chip = chip_mate(d) // CORES

            def both(k, _):
                for c in range(CORES):
                    start_kv(chip * CORES + c)(k, 0)
                return 0

            lax.fori_loop(0, chunks, both, 0)

    kv_across()
    remote(patches, pbuf.at[rows_of(s)], p_send.at[0], rest_recv.at[0], seq=partner).start()
    lax.fori_loop(0, chunks, start_kv(partner), 0)
    pl.when(jnp.logical_not(far))(kv_beside)

    row_mate = f + 1 - 2 * lax.rem(f, GRID)
    column_mate = lax.rem(f + GRID, fn)

    def weight_copy(pair, recv, start, size, to):
        at = pl.ds(pl.multiple_of(start, size), size)
        return remote(wbuf.at[pair, at], wbuf.at[pair, at], w_send.at[0], recv.at[pair], fsdp=to)

    def near_start(pair):
        weight_copy(pair, near_recv, f * rows, rows, row_mate).start()
        weight_copy(pair, near_recv, f * rows, rows, column_mate).start()

    def relay(pair):
        part = rows // 2
        drain(wbuf.at[pair, pl.ds(0, 2 * rows)], near_recv.at[pair])
        weight_copy(pair, relay_recv, row_mate * rows, part, column_mate).start()
        weight_copy(pair, relay_recv, column_mate * rows + part, part, row_mate).start()

    drain(scales, scale_sem.at[0])
    drain(cbuf, code_sem.at[0])

    def dequantize_pair(pair, _):
        for side in range(2):
            q = 2 * pair + side
            for block in range(rows // BLOCK):
                scale = scales[block, chunk_column(q) // BLOCK]
                piece = cbuf[q, block * BLOCK:(block + 1) * BLOCK, :].astype(jnp.float32) * scale
                at = pl.ds(pl.multiple_of(f * rows + block * BLOCK, BLOCK), BLOCK)
                wbuf[pair, at, side * LANES:(side + 1) * LANES] = piece.astype(jnp.bfloat16)

        @pl.when(pair < chunks - 1)
        def _():
            near_start(pair)

        return 0

    lax.fori_loop(0, chunks, dequantize_pair, 0)

    for pair in range(chunks - 1):
        relay(pair)
    near_start(chunks - 1)

    for d in range(1, chips):
        at = rows_of(half * m + lax.rem(place + m - d * CORES, m))
        drain(pbuf.at[at], mate_recv.at[d - 1])
        remote(pbuf.at[at], pbuf.at[at], p_send.at[0], rest_recv.at[0], seq=partner).start()
    drain(gains, gain_sem.at[0])
    drain(pbuf.at[pl.ds(0, (chips + 1) * tokens)], rest_recv.at[0])

    other = lax.rem(s + m, n)
    half_rows = pl.ds(pl.multiple_of(half * group, group), group)

    def query_copy(k):
        return remote(qsend.at[k], qbuf.at[k, half_rows], q_send.at[0], q_recv.at[k], seq=other)

    def project(pair):
        drain(wbuf.at[pair, pl.ds(0, rows)], relay_recv.at[pair])
        both = jnp.dot(pbuf[...], wbuf[pair], preferred_element_type=jnp.float32)
        for side in range(2):
            q = 2 * pair + side
            normed = column_norm(
                both[:, side * LANES:(side + 1) * LANES], gains[0, :, pl.ds(chunk_column(q), LANES)])
            if q < chunks:
                qsend[q] = normed
                query_copy(q).start()
            else:
                qbuf[q - chunks, half_rows] = normed

    for pair in range(chunks - 1):
        project(pair)
    pl.when(far)(kv_beside)
    relay(chunks - 1)
    project(chunks - 1)

    tile = CORES * tokens
    exponent = HDIM ** (-0.5) * math.log2(math.e)

    def out_copy(k, to):
        return remote(obuf.at[k, all_rows_of(to)], out.at[:, owned_chunk(s, k)], o_send.at[0], o_recv.at[0], seq=to)

    first = lax.broadcasted_iota(jnp.int32, (tile, LANES), 1) < HDIM
    last = 2 * chunks - 1

    def attend_step(step, _):
        g, i = step // chips, lax.rem(step, chips)
        mine = jnp.logical_or(jnp.logical_and(g > 0, lax.rem(g, 2) == 0), g == last)
        k = jnp.where(g == 0, 0, jnp.where(mine, (g - 1) // 2, (g + 1) // 2))
        own_side = half * chips + lax.rem(place // CORES + 1 + i, chips)
        chip = jnp.where(mine, own_side, (1 - half) * chips + i)
        here = pl.ds(pl.multiple_of(chip * tile, tile), tile)

        @pl.when(jnp.logical_and(i == 0, jnp.logical_not(mine)))
        def _():
            drain(kv.at[k], kv_recv.at[k])
            kv[k, 0] = column_norm(kv[k, 0].astype(jnp.float32), gains[1, :, owned_chunk(s, k)])
            query_copy(k).wait_recv()

        values = kv[k, 1]
        keys = kv[k, 0]
        queries = qbuf[k, here]
        results = []
        for mask in (first, jnp.logical_not(first)):
            masked = jnp.where(mask, queries, jnp.zeros_like(queries))
            scores = lax.dot_general(
                masked, keys, (((1,), (1,)), ((), ())), preferred_element_type=jnp.float32)
            largest = jnp.max(scores, axis=-1, keepdims=True)
            probability = jnp.exp2((scores - largest) * exponent)
            normaliser = jnp.sum(probability, axis=-1, keepdims=True)
            blended = jnp.dot(
                probability.astype(jnp.bfloat16), values, preferred_element_type=jnp.float32)
            results.append(blended / normaliser)
        obuf[k, here] = jnp.where(first, results[0], results[1]).astype(jnp.bfloat16)
        for c in range(CORES):
            to = chip * CORES + c

            @pl.when(to != s)
            def _():
                out_copy(k, to).start()

            @pl.when(to == s)
            def _():
                out[:, owned_chunk(s, k)] = obuf[k, all_rows_of(s)]

        return 0

    lax.fori_loop(0, 2 * chunks * chips, attend_step, 0)

    drain(pbuf.at[pl.ds(0, (2 * chips - 1) * tokens)], p_send.at[0])
    drain(wbuf.at[:, pl.ds(0, 3 * rows)], w_send.at[0])
    drain(kv.at[:, :, pl.ds(0, (n - 1) * tokens)], kv_send.at[0])
    drain(qsend, q_send.at[0])
    drain(obuf.at[:, pl.ds(0, (n - 1) * tokens)], o_send.at[0])
    drain(out.at[:, pl.ds(0, (n - 1) * width)], o_recv.at[0])


def fused_per_device(n, fn, patches, weight_codes, block_scales, key_proj, value_proj, query_gain, key_gain):
    _, tokens, features = patches.shape
    rows, columns = weight_codes.shape
    width = columns // n
    chunks = width // LANES
    group = n // 2 * tokens
    chips = n // 2 // CORES
    bf16 = jnp.bfloat16
    dma = pltpu.SemaphoreType.DMA
    anywhere = pl.BlockSpec(memory_space=pl.ANY)
    result = pl.pallas_call(
        functools.partial(fused_kernel, n, fn),
        out_shape=pltpu.VMEM((tokens, columns), bf16),
        in_specs=[anywhere] * 7,
        out_specs=pl.BlockSpec(memory_space=pltpu.VMEM),
        scratch_shapes=[
            pltpu.VMEM((group, features), bf16),
            pltpu.VMEM((2 * chunks, rows, LANES), jnp.int32),
            pltpu.VMEM((chunks, features, 2 * LANES), bf16),
            pltpu.VMEM((chunks, 2, n * tokens, LANES), bf16),
            pltpu.VMEM((chunks, group, LANES), bf16),
            pltpu.VMEM((chunks, n * tokens, LANES), bf16),
            pltpu.VMEM((chunks, n * tokens, LANES), bf16),
            pltpu.VMEM((2, 1, columns), jnp.float32),
            pltpu.SMEM(block_scales.shape, jnp.float32),
            dma((1,)), dma((1,)), dma((1,)), dma((chips - 1,)), dma((1,)), dma((1,)),
            dma((chunks,)), dma((chunks,)), dma((1,)),
            dma((1,)), dma((chunks,)), dma((1,)), dma((chunks,)), dma((1,)), dma((1,)),
        ],
        compiler_params=pltpu.CompilerParams(
            collective_id=0, has_side_effects=True, vmem_limit_bytes=56 * 1024 * 1024),
    )(
        patches.reshape(tokens, features), weight_codes, block_scales,
        key_proj.reshape(tokens, columns), value_proj.reshape(tokens, columns),
        query_gain.reshape(1, columns), key_gain.reshape(1, columns),
    )
    return result.reshape(1, tokens, columns)


def solution(mesh):
    n, fn = mesh.shape["seq"], mesh.shape["fsdp"]
    specs = (
        P("fsdp", "seq", None), P("fsdp", None), P("fsdp", None),
        P("fsdp", "seq", None), P("fsdp", "seq", None), P(), P(),
    )

    def whole(*arrays):
        patches, weight_codes = arrays[:2]
        fits = patches.shape[0] == fn == GRID * GRID and weight_codes.shape[1] % (n * LANES) == 0 and n % (2 * CORES) == 0 and n > 2 * CORES
        body = functools.partial(fused_per_device, n, fn) if fits else per_device
        return jax.shard_map(
            body, mesh=mesh, in_specs=specs, out_specs=P("fsdp", "seq", None), check_vma=False
        )(*arrays)

    return whole
```

time: 77.8 us -> 75.9 us (0.976); the launches traced: 77.6 us -> 74.6 us
  Pallas kernels: 76.7 us -> 73.7 us
    pallas_call x1, Pallas kernels: 76.7 us -> 73.7 us  [fused_per_device(): pl.pallas_call(functools.partial(fused_kernel, n, fn), out_shape=pltpu.VM...]
where the time goes in v1:
time: 75.9 us; the launch traced here: 74.6 us
  Pallas kernels  73.7 us (97%)
  local copies, waits for them, and re-layouts  0.88 us (1%)
    pallas_call x1, Pallas kernels, fused_per_device(): pl.pallas_call(functools.partial(fused_kernel, n, fn), out_shape=pltpu.VM...  73.7 us

profile of v1, /device:TPU:0, one launch (start us, length us, event | category | flops | bytes accessed | tf_op | source)
XLA Modules:
  0.0 74.6 jit_solution(7218843037999876570)
XLA Ops:
  0.0 73.7 %shard_map.73 = bf16[128,3072]{1,0:T(8,128)(2,1)S(1)} custom-call(bf16[128,3072]{1,0:T(8,128)(2,1)} %bitcast.7, s32[768,3072]{1,0:T(8,128)} %codes.1, f32[6,24]{1,0:T(8,128)} %scales_in.1, bf16[128,3072]{1,0:T(8,128)(2,1)} %bitcast.8, bf16[128,3072]{1,0:T(8,128)(2,1)} %bitcast.9, f32[1,3072]{1,0:T(1,128)} %bitcast.10, f32[1,3072]{1,0:T(1,128)} %bitcast.11), custom_call_target="tpu_custom_call" | custom-call | tf_op jit(solution)/shard_map/pallas_call | solution.py:367
  73.8 0.9 %copy.9 = bf16[1,128,3072]{2,1,0:T(8,128)(2,1)} copy(bf16[1,128,3072]{2,1,0:T(8,128)(2,1)S(1)} %bitcast.6) | data formatting | bytes 1572864

commit v2 on v1

--- a/solution.py
+++ b/solution.py
@@ -112,10 +112,22 @@
     return normed.astype(jnp.bfloat16)
 
 
+def attend_order(chunks, chips):
+    order, late = [], []
+    for k in range(chunks):
+        order += [(0, k, i, int(i == 0)) for i in range(chips if k == 0 else 1)]
+        order += late
+        late = [(0, k, i, 0) for i in range(1, chips)] if k > 0 else []
+        if k == chunks - 1:
+            order += late
+        order += [(1, k, i, 0) for i in range(chips)]
+    return order
+
+
 def fused_kernel(
     n, fn, patches, codes, scales_in, key, value, query_gain_in, key_gain_in, out,
-    pbuf, cbuf, wbuf, kv, qsend, qbuf, obuf, gains, scales,
-    code_sem, scale_sem, gain_sem, mate_recv, rest_recv, p_send, near_recv, relay_recv, w_send,
+    pbuf, cbuf, wbuf, own, kv, qsend, qbuf, obuf, gains, scales,
+    own_sem, code_sem, scale_sem, gain_sem, mate_recv, rest_recv, p_send, near_recv, relay_recv, w_send,
     kv_send, kv_recv, q_send, q_recv, o_send, o_recv,
 ):
     s, f = lax.axis_index("seq"), lax.axis_index("fsdp")
@@ -158,67 +170,66 @@
     def drain(ref, sem):
         pltpu.make_async_copy(ref, ref, sem).wait()
 
+    pltpu.make_async_copy(patches, pbuf.at[rows_of(s)], own_sem.at[0]).start()
+    for which, src in enumerate((key, value)):
+        pltpu.make_async_copy(src, own.at[which], own_sem.at[1]).start()
     pltpu.make_async_copy(scales_in, scales, scale_sem.at[0]).start()
     for q in range(2 * chunks):
         pltpu.make_async_copy(codes.at[:, pl.ds(chunk_column(q), LANES)], cbuf.at[q], code_sem.at[0]).start()
-    pltpu.make_async_copy(patches, pbuf.at[rows_of(s)], rest_recv.at[0]).start()
+
+    pl.semaphore_wait(barrier, n - 1 + fn - 1)
+    drain(pbuf.at[rows_of(s)], own_sem.at[0])
+
+    def remote(src, dst, send, recv, **device):
+        return pltpu.make_async_remote_copy(
+            src_ref=src, dst_ref=dst, send_sem=send, recv_sem=recv, device_id=device, device_id_type=MESH)
+
+    def mate_copy(d):
+        return remote(pbuf.at[rows_of(s)], pbuf.at[rows_of(s)], p_send.at[0], mate_recv.at[d - 1], seq=chip_mate(d))
+
+    for d in range(1, chips):
+        mate_copy(d).start()
+
+    far = place // CORES == jnp.where(half == 0, 0, chips - 1)
+
+    def start_kv(to):
+        def one(k, _):
+            for which in range(2):
+                remote(
+                    own.at[which, :, owned_chunk(to, k)], kv.at[k, which, all_rows_of(s)],
+                    kv_send.at[0], kv_recv.at[k], seq=to).start()
+            return 0
+
+        return one
+
+    def start_chip(chip, low, high):
+        def both(k, _):
+            for c in range(CORES):
+                start_kv(chip * CORES + c)(k, 0)
+            return 0
+
+        lax.fori_loop(low, high, both, 0)
+
+    def across(j):
+        return jnp.where(half == 0, chips + j, chips - 1 - j)
+
+    def beside(low, high):
+        for d in range(1, chips):
+            start_chip(chip_mate(d) // CORES, low, high)
+
+    drain(own, own_sem.at[1])
+    start_chip(across(0), 0, chunks)
     pltpu.make_async_copy(query_gain_in, gains.at[0], gain_sem.at[0]).start()
     pltpu.make_async_copy(key_gain_in, gains.at[1], gain_sem.at[0]).start()
     for k in range(chunks):
         for which, src in enumerate((key, value)):
             pltpu.make_async_copy(
                 src.at[:, owned_chunk(s, k)], kv.at[k, which, all_rows_of(s)], kv_recv.at[k]).start()
-
-    pl.semaphore_wait(barrier, n - 1 + fn - 1)
-
-    def remote(src, dst, send, recv, **device):
-        return pltpu.make_async_remote_copy(
-            src_ref=src, dst_ref=dst, send_sem=send, recv_sem=recv, device_id=device, device_id_type=MESH)
-
-    def mate_copy(d):
-        return remote(patches, pbuf.at[rows_of(s)], p_send.at[0], mate_recv.at[d - 1], seq=chip_mate(d))
-
-    for d in range(1, chips):
-        mate_copy(d).start()
-
-    far = place // CORES == jnp.where(half == 0, 0, chips - 1)
-
-    def start_kv(to):
-        def one(k, _):
-            for which, src in enumerate((key, value)):
-                remote(
-                    src.at[:, owned_chunk(to, k)], kv.at[k, which, all_rows_of(s)],
-                    kv_send.at[0], kv_recv.at[k], seq=to).start()
-            return 0
-
-        return one
-
-    def kv_across():
-        for j in range(chips):
-            chip = jnp.where(half == 0, chips + j, chips - 1 - j)
-
-            def both(k, _):
-                for c in range(CORES):
-                    start_kv(chip * CORES + c)(k, 0)
-                return 0
-
-            lax.fori_loop(0, chunks, both, 0)
-
-    def kv_beside():
-        for d in range(1, chips):
-            chip = chip_mate(d) // CORES
-
-            def both(k, _):
-                for c in range(CORES):
-                    start_kv(chip * CORES + c)(k, 0)
-                return 0
-
-            lax.fori_loop(0, chunks, both, 0)
-
-    kv_across()
-    remote(patches, pbuf.at[rows_of(s)], p_send.at[0], rest_recv.at[0], seq=partner).start()
+    pl.when(far)(lambda: beside(0, 1))
+    for j in range(1, chips):
+        start_chip(across(j), 0, chunks)
+    remote(pbuf.at[rows_of(s)], pbuf.at[rows_of(s)], p_send.at[0], rest_recv.at[0], seq=partner).start()
     lax.fori_loop(0, chunks, start_kv(partner), 0)
-    pl.when(jnp.logical_not(far))(kv_beside)
 
     row_mate = f + 1 - 2 * lax.rem(f, GRID)
     column_mate = lax.rem(f + GRID, fn)
@@ -227,12 +238,13 @@
         at = pl.ds(pl.multiple_of(start, size), size)
         return remote(wbuf.at[pair, at], wbuf.at[pair, at], w_send.at[0], recv.at[pair], fsdp=to)
 
-    def near_start(pair):
-        weight_copy(pair, near_recv, f * rows, rows, row_mate).start()
-        weight_copy(pair, near_recv, f * rows, rows, column_mate).start()
+    part = rows // 2
+
+    def near_start(pair, start, size):
+        for mate in (row_mate, column_mate):
+            weight_copy(pair, near_recv, f * rows + start, size, mate).start()
 
     def relay(pair):
-        part = rows // 2
         drain(wbuf.at[pair, pl.ds(0, 2 * rows)], near_recv.at[pair])
         weight_copy(pair, relay_recv, row_mate * rows, part, column_mate).start()
         weight_copy(pair, relay_recv, column_mate * rows + part, part, row_mate).start()
@@ -249,24 +261,35 @@
                 at = pl.ds(pl.multiple_of(f * rows + block * BLOCK, BLOCK), BLOCK)
                 wbuf[pair, at, side * LANES:(side + 1) * LANES] = piece.astype(jnp.bfloat16)
 
-        @pl.when(pair < chunks - 1)
+        @pl.when(pair == 0)
         def _():
-            near_start(pair)
+            near_start(pair, 0, rows)
+
+        @pl.when(pair == 1)
+        def _():
+            near_start(pair, 0, part)
 
         return 0
 
     lax.fori_loop(0, chunks, dequantize_pair, 0)
 
-    for pair in range(chunks - 1):
-        relay(pair)
-    near_start(chunks - 1)
-
-    for d in range(1, chips):
-        at = rows_of(half * m + lax.rem(place + m - d * CORES, m))
-        drain(pbuf.at[at], mate_recv.at[d - 1])
-        remote(pbuf.at[at], pbuf.at[at], p_send.at[0], rest_recv.at[0], seq=partner).start()
+    def patches_in():
+        for d in range(1, chips):
+            at = rows_of(half * m + lax.rem(place + m - d * CORES, m))
+            drain(pbuf.at[at], mate_recv.at[d - 1])
+            remote(pbuf.at[at], pbuf.at[at], p_send.at[0], rest_recv.at[0], seq=partner).start()
+        drain(pbuf.at[pl.ds(0, chips * tokens)], rest_recv.at[0])
+
+    def relay_rest():
+        for pair in range(1, chunks - 1):
+            relay(pair)
+            near_start(pair + 1, 0, rows)
+
+    relay(0)
+    near_start(1, part, part)
+    pl.when(far)(relay_rest)
+    patches_in()
     drain(gains, gain_sem.at[0])
-    drain(pbuf.at[pl.ds(0, (chips + 1) * tokens)], rest_recv.at[0])
 
     other = lax.rem(s + m, n)
     half_rows = pl.ds(pl.multiple_of(half * group, group), group)
@@ -287,9 +310,11 @@
             else:
                 qbuf[q - chunks, half_rows] = normed
 
-    for pair in range(chunks - 1):
+    project(0)
+    pl.when(jnp.logical_not(far))(relay_rest)
+    for pair in range(1, chunks - 1):
         project(pair)
-    pl.when(far)(kv_beside)
+    beside(jnp.where(far, 1, 0), chunks)
     relay(chunks - 1)
     project(chunks - 1)
 
@@ -300,17 +325,19 @@
         return remote(obuf.at[k, all_rows_of(to)], out.at[:, owned_chunk(s, k)], o_send.at[0], o_recv.at[0], seq=to)
 
     first = lax.broadcasted_iota(jnp.int32, (tile, LANES), 1) < HDIM
-    last = 2 * chunks - 1
+
+    order = attend_order(chunks, chips)
+
+    def entry(step, column):
+        return sum(jnp.where(step == at, row[column], 0) for at, row in enumerate(order))
 
     def attend_step(step, _):
-        g, i = step // chips, lax.rem(step, chips)
-        mine = jnp.logical_or(jnp.logical_and(g > 0, lax.rem(g, 2) == 0), g == last)
-        k = jnp.where(g == 0, 0, jnp.where(mine, (g - 1) // 2, (g + 1) // 2))
+        mine, k, i, opens = (entry(step, column) for column in range(4))
         own_side = half * chips + lax.rem(place // CORES + 1 + i, chips)
-        chip = jnp.where(mine, own_side, (1 - half) * chips + i)
+        chip = jnp.where(mine == 1, own_side, across(chips - 1 - i))
         here = pl.ds(pl.multiple_of(chip * tile, tile), tile)
 
-        @pl.when(jnp.logical_and(i == 0, jnp.logical_not(mine)))
+        @pl.when(opens == 1)
         def _():
             drain(kv.at[k], kv_recv.at[k])
             kv[k, 0] = column_norm(kv[k, 0].astype(jnp.float32), gains[1, :, owned_chunk(s, k)])
@@ -344,7 +371,7 @@
 
         return 0
 
-    lax.fori_loop(0, 2 * chunks * chips, attend_step, 0)
+    lax.fori_loop(0, len(order), attend_step, 0)
 
     drain(pbuf.at[pl.ds(0, (2 * chips - 1) * tokens)], p_send.at[0])
     drain(wbuf.at[:, pl.ds(0, 3 * rows)], w_send.at[0])
@@ -373,13 +400,14 @@
             pltpu.VMEM((group, features), bf16),
             pltpu.VMEM((2 * chunks, rows, LANES), jnp.int32),
             pltpu.VMEM((chunks, features, 2 * LANES), bf16),
+            pltpu.VMEM((2, tokens, columns), bf16),
             pltpu.VMEM((chunks, 2, n * tokens, LANES), bf16),
             pltpu.VMEM((chunks, group, LANES), bf16),
             pltpu.VMEM((chunks, n * tokens, LANES), bf16),
             pltpu.VMEM((chunks, n * tokens, LANES), bf16),
             pltpu.VMEM((2, 1, columns), jnp.float32),
             pltpu.SMEM(block_scales.shape, jnp.float32),
-            dma((1,)), dma((1,)), dma((1,)), dma((chips - 1,)), dma((1,)), dma((1,)),
+            dma((2,)), dma((1,)), dma((1,)), dma((1,)), dma((chips - 1,)), dma((1,)), dma((1,)),
             dma((chunks,)), dma((chunks,)), dma((1,)),
             dma((1,)), dma((chunks,)), dma((1,)), dma((chunks,)), dma((1,)), dma((1,)),
         ],

time: 75.9 us -> 74.2 us (0.978)
  Pallas kernels: 73.7 us -> 72.2 us
    pallas_call x1, Pallas kernels: 73.7 us -> 72.2 us  [fused_per_device(): pl.pallas_call(functools.partial(fused_kernel, n, fn), out_shape=pltpu.VM...]
where the time goes in v2:
time: 74.2 us; the launch traced here: 73.1 us
  Pallas kernels  72.2 us (97%)
  local copies, waits for them, and re-layouts  0.88 us (1%)
    pallas_call x1, Pallas kernels, fused_per_device(): pl.pallas_call(functools.partial(fused_kernel, n, fn), out_shape=pltpu.VM...  72.2 us

profile of v2, /device:TPU:0, one launch (start us, length us, event | category | flops | bytes accessed | tf_op | source)
XLA Modules:
  0.0 73.1 jit_solution(2447483574206749025)
XLA Ops:
  0.0 72.2 %shard_map.73 = bf16[128,3072]{1,0:T(8,128)(2,1)S(1)} custom-call(bf16[128,3072]{1,0:T(8,128)(2,1)} %bitcast.7, s32[768,3072]{1,0:T(8,128)} %codes.1, f32[6,24]{1,0:T(8,128)} %scales_in.1, bf16[128,3072]{1,0:T(8,128)(2,1)} %bitcast.8, bf16[128,3072]{1,0:T(8,128)(2,1)} %bitcast.9, f32[1,3072]{1,0:T(1,128)} %bitcast.10, f32[1,3072]{1,0:T(1,128)} %bitcast.11), custom_call_target="tpu_custom_call" | custom-call | tf_op jit(solution)/shard_map/pallas_call | solution.py:394
  72.2 0.9 %copy.9 = bf16[1,128,3072]{2,1,0:T(8,128)(2,1)} copy(bf16[1,128,3072]{2,1,0:T(8,128)(2,1)S(1)} %bitcast.6) | data formatting | bytes 1572864

commit v3 on v2

--- a/solution.py
+++ b/solution.py
@@ -127,8 +127,8 @@
 def fused_kernel(
     n, fn, patches, codes, scales_in, key, value, query_gain_in, key_gain_in, out,
     pbuf, cbuf, wbuf, own, kv, qsend, qbuf, obuf, gains, scales,
-    own_sem, code_sem, scale_sem, gain_sem, mate_recv, rest_recv, p_send, near_recv, relay_recv, w_send,
-    kv_send, kv_recv, q_send, q_recv, o_send, o_recv,
+    own_sem, code_sem, scale_sem, gain_sem, mate_recv, rest_recv, p_send, first_recv, rest_w_recv, w_send,
+    kv_send, kv_recv, q_send, q_recv, o_send, o_recv, met,
 ):
     s, f = lax.axis_index("seq"), lax.axis_index("fsdp")
     m = n // 2
@@ -143,13 +143,33 @@
     partner = s + 1 - 2 * core
 
     barrier = pltpu.get_barrier_semaphore()
-    for d in range(1, n):
-        pl.semaphore_signal(barrier, inc=1, device_id={"seq": lax.rem(s + d, n)}, device_id_type=MESH)
-    for d in range(1, fn):
-        pl.semaphore_signal(barrier, inc=1, device_id={"fsdp": lax.rem(f + d, fn)}, device_id_type=MESH)
-
-    def chip_mate(d):
-        return half * m + lax.rem(place + d * CORES, m)
+    far = place // CORES == jnp.where(half == 0, 0, chips - 1)
+    near = jnp.logical_not(far)
+    row_mate = f + 1 - 2 * lax.rem(f, GRID)
+    column_mate = lax.rem(f + GRID, fn)
+
+    beside_device = half * m + lax.rem(place + CORES, m)
+    def across(j):
+        return jnp.where(half == 0, chips + j, chips - 1 - j)
+
+    def greet(semaphore, chip):
+        for c in range(CORES):
+            pl.semaphore_signal(semaphore, inc=1, device_id={"seq": chip * CORES + c}, device_id_type=MESH)
+
+    beside_chip = beside_device // CORES
+
+    @pl.when(near)
+    def _():
+        greet(barrier, across(0))
+        greet(barrier, beside_chip)
+
+    @pl.when(jnp.logical_and(far, half == 1))
+    def _():
+        greet(barrier, beside_chip)
+
+    pl.semaphore_signal(barrier, inc=1, device_id={"seq": partner}, device_id_type=MESH)
+    for mate in (row_mate, column_mate):
+        pl.semaphore_signal(barrier, inc=1, device_id={"fsdp": mate}, device_id_type=MESH)
 
     def rows_of(device):
         return pl.ds(pl.multiple_of(lax.rem(device, m) * tokens, tokens), tokens)
@@ -177,62 +197,64 @@
     for q in range(2 * chunks):
         pltpu.make_async_copy(codes.at[:, pl.ds(chunk_column(q), LANES)], cbuf.at[q], code_sem.at[0]).start()
 
-    pl.semaphore_wait(barrier, n - 1 + fn - 1)
-    drain(pbuf.at[rows_of(s)], own_sem.at[0])
+    pl.semaphore_wait(barrier, CORES + 3 + jnp.where(jnp.logical_and(near, half == 1), CORES, 0))
 
     def remote(src, dst, send, recv, **device):
         return pltpu.make_async_remote_copy(
             src_ref=src, dst_ref=dst, send_sem=send, recv_sem=recv, device_id=device, device_id_type=MESH)
 
-    def mate_copy(d):
-        return remote(pbuf.at[rows_of(s)], pbuf.at[rows_of(s)], p_send.at[0], mate_recv.at[d - 1], seq=chip_mate(d))
-
-    for d in range(1, chips):
-        mate_copy(d).start()
-
-    far = place // CORES == jnp.where(half == 0, 0, chips - 1)
+    def mate_copy():
+        return remote(pbuf.at[rows_of(s)], pbuf.at[rows_of(s)], p_send.at[0], mate_recv.at[0], seq=beside_device)
 
     def start_kv(to):
-        def one(k, _):
-            for which in range(2):
-                remote(
-                    own.at[which, :, owned_chunk(to, k)], kv.at[k, which, all_rows_of(s)],
-                    kv_send.at[0], kv_recv.at[k], seq=to).start()
+        def one(unit, _):
+            k, which = unit // 2, lax.rem(unit, 2)
+            remote(
+                own.at[which, :, owned_chunk(to, k)], kv.at[k, which, all_rows_of(s)],
+                kv_send.at[0], kv_recv.at[k], seq=to).start()
             return 0
 
         return one
 
     def start_chip(chip, low, high):
-        def both(k, _):
+        def both(unit, _):
             for c in range(CORES):
-                start_kv(chip * CORES + c)(k, 0)
+                start_kv(chip * CORES + c)(unit, 0)
             return 0
 
         lax.fori_loop(low, high, both, 0)
 
-    def across(j):
-        return jnp.where(half == 0, chips + j, chips - 1 - j)
+    early_units = jnp.where(half == 0, 3, 2)
 
     def beside(low, high):
-        for d in range(1, chips):
-            start_chip(chip_mate(d) // CORES, low, high)
-
-    drain(own, own_sem.at[1])
-    start_chip(across(0), 0, chunks)
-    pltpu.make_async_copy(query_gain_in, gains.at[0], gain_sem.at[0]).start()
-    pltpu.make_async_copy(key_gain_in, gains.at[1], gain_sem.at[0]).start()
+        start_chip(beside_chip, low, high)
+
+    @pl.when(near)
+    def _():
+        drain(own, own_sem.at[1])
+        start_chip(across(0), 0, 2 * chunks)
+
+        @pl.when(half == 0)
+        def _():
+            pl.semaphore_wait(met.at[1], CORES)
+
+        greet(met.at[0], beside_chip)
+        greet(met.at[2], across(0))
+        drain(pbuf.at[rows_of(s)], own_sem.at[0])
+        mate_copy().start()
+
+    @pl.when(far)
+    def _():
+        pl.when(half == 0)(lambda: greet(met.at[1], beside_chip))
+        drain(pbuf.at[rows_of(s)], own_sem.at[0])
+        mate_copy().start()
+
     for k in range(chunks):
         for which, src in enumerate((key, value)):
             pltpu.make_async_copy(
                 src.at[:, owned_chunk(s, k)], kv.at[k, which, all_rows_of(s)], kv_recv.at[k]).start()
-    pl.when(far)(lambda: beside(0, 1))
-    for j in range(1, chips):
-        start_chip(across(j), 0, chunks)
-    remote(pbuf.at[rows_of(s)], pbuf.at[rows_of(s)], p_send.at[0], rest_recv.at[0], seq=partner).start()
-    lax.fori_loop(0, chunks, start_kv(partner), 0)
-
-    row_mate = f + 1 - 2 * lax.rem(f, GRID)
-    column_mate = lax.rem(f + GRID, fn)
+    pltpu.make_async_copy(query_gain_in, gains.at[0], gain_sem.at[0]).start()
+    pltpu.make_async_copy(key_gain_in, gains.at[1], gain_sem.at[0]).start()
 
     def weight_copy(pair, recv, start, size, to):
         at = pl.ds(pl.multiple_of(start, size), size)
@@ -240,14 +262,15 @@
 
     part = rows // 2
 
-    def near_start(pair, start, size):
-        for mate in (row_mate, column_mate):
-            weight_copy(pair, near_recv, f * rows + start, size, mate).start()
+    def weights_out(pair):
+        for recv, row_half in ((first_recv, 0), (rest_w_recv, part)):
+            weight_copy(pair, recv, f * rows + row_half, part, row_mate).start()
+            weight_copy(pair, recv, f * rows + part - row_half, part, column_mate).start()
 
     def relay(pair):
-        drain(wbuf.at[pair, pl.ds(0, 2 * rows)], near_recv.at[pair])
-        weight_copy(pair, relay_recv, row_mate * rows, part, column_mate).start()
-        weight_copy(pair, relay_recv, column_mate * rows + part, part, row_mate).start()
+        drain(wbuf.at[pair, pl.ds(0, rows)], first_recv.at[pair])
+        weight_copy(pair, rest_w_recv, row_mate * rows, part, column_mate).start()
+        weight_copy(pair, rest_w_recv, column_mate * rows + part, part, row_mate).start()
 
     drain(scales, scale_sem.at[0])
     drain(cbuf, code_sem.at[0])
@@ -261,35 +284,42 @@
                 at = pl.ds(pl.multiple_of(f * rows + block * BLOCK, BLOCK), BLOCK)
                 wbuf[pair, at, side * LANES:(side + 1) * LANES] = piece.astype(jnp.bfloat16)
 
-        @pl.when(pair == 0)
-        def _():
-            near_start(pair, 0, rows)
-
-        @pl.when(pair == 1)
-        def _():
-            near_start(pair, 0, part)
-
+        pl.when(pair == 0)(lambda: weights_out(0))
         return 0
 
     lax.fori_loop(0, chunks, dequantize_pair, 0)
 
-    def patches_in():
-        for d in range(1, chips):
-            at = rows_of(half * m + lax.rem(place + m - d * CORES, m))
-            drain(pbuf.at[at], mate_recv.at[d - 1])
-            remote(pbuf.at[at], pbuf.at[at], p_send.at[0], rest_recv.at[0], seq=partner).start()
-        drain(pbuf.at[pl.ds(0, chips * tokens)], rest_recv.at[0])
-
-    def relay_rest():
-        for pair in range(1, chunks - 1):
-            relay(pair)
-            near_start(pair + 1, 0, rows)
+    @pl.when(near)
+    def _():
+        pl.semaphore_wait(met.at[2], CORES)
+        greet(met.at[3], beside_chip)
+
+    @pl.when(far)
+    def _():
+        drain(own, own_sem.at[1])
+        pl.semaphore_wait(met.at[0], CORES)
+        start_chip(across(0), 0, 2 * chunks)
+        beside(0, early_units)
+        pl.semaphore_wait(met.at[3], CORES)
+
+    start_chip(across(1), 0, 2 * chunks)
+    remote(pbuf.at[rows_of(s)], pbuf.at[rows_of(s)], p_send.at[0], rest_recv.at[0], seq=partner).start()
+    lax.fori_loop(0, 2 * chunks, start_kv(partner), 0)
+
+    def forward():
+        at = rows_of(beside_device)
+        drain(pbuf.at[at], mate_recv.at[0])
+        remote(pbuf.at[at], pbuf.at[at], p_send.at[0], rest_recv.at[0], seq=partner).start()
 
     relay(0)
-    near_start(1, part, part)
-    pl.when(far)(relay_rest)
-    patches_in()
+    weights_out(1)
+    pl.when(near)(forward)
+    for pair in range(1, chunks - 1):
+        relay(pair)
+        weights_out(pair + 1)
+    pl.when(far)(forward)
     drain(gains, gain_sem.at[0])
+    drain(pbuf.at[pl.ds(0, chips * tokens)], rest_recv.at[0])
 
     other = lax.rem(s + m, n)
     half_rows = pl.ds(pl.multiple_of(half * group, group), group)
@@ -298,7 +328,7 @@
         return remote(qsend.at[k], qbuf.at[k, half_rows], q_send.at[0], q_recv.at[k], seq=other)
 
     def project(pair):
-        drain(wbuf.at[pair, pl.ds(0, rows)], relay_recv.at[pair])
+        drain(wbuf.at[pair, pl.ds(0, 2 * rows)], rest_w_recv.at[pair])
         both = jnp.dot(pbuf[...], wbuf[pair], preferred_element_type=jnp.float32)
         for side in range(2):
             q = 2 * pair + side
@@ -310,11 +340,9 @@
             else:
                 qbuf[q - chunks, half_rows] = normed
 
-    project(0)
-    pl.when(jnp.logical_not(far))(relay_rest)
-    for pair in range(1, chunks - 1):
+    for pair in range(chunks - 1):
         project(pair)
-    beside(jnp.where(far, 1, 0), chunks)
+    beside(jnp.where(far, early_units, 0), 2 * chunks)
     relay(chunks - 1)
     project(chunks - 1)
 
@@ -407,9 +435,10 @@
             pltpu.VMEM((chunks, n * tokens, LANES), bf16),
             pltpu.VMEM((2, 1, columns), jnp.float32),
             pltpu.SMEM(block_scales.shape, jnp.float32),
-            dma((2,)), dma((1,)), dma((1,)), dma((1,)), dma((chips - 1,)), dma((1,)), dma((1,)),
+            dma((2,)), dma((1,)), dma((1,)), dma((1,)), dma((1,)), dma((1,)), dma((1,)),
             dma((chunks,)), dma((chunks,)), dma((1,)),
             dma((1,)), dma((chunks,)), dma((1,)), dma((chunks,)), dma((1,)), dma((1,)),
+            pltpu.SemaphoreType.REGULAR((4,)),
         ],
         compiler_params=pltpu.CompilerParams(
             collective_id=0, has_side_effects=True, vmem_limit_bytes=56 * 1024 * 1024),
@@ -430,7 +459,7 @@
 
     def whole(*arrays):
         patches, weight_codes = arrays[:2]
-        fits = patches.shape[0] == fn == GRID * GRID and weight_codes.shape[1] % (n * LANES) == 0 and n % (2 * CORES) == 0 and n > 2 * CORES
+        fits = patches.shape[0] == fn == GRID * GRID and weight_codes.shape[1] % (n * LANES) == 0 and n == 2 * GRID * CORES
         body = functools.partial(fused_per_device, n, fn) if fits else per_device
         return jax.shard_map(
             body, mesh=mesh, in_specs=specs, out_specs=P("fsdp", "seq", None), check_vma=False

time: 74.2 us -> 73.7 us (level)
  no operation moved by 1% of the time
where the time goes in v3:
time: 73.7 us; the launch traced here: 72.6 us
  Pallas kernels  71.7 us (97%)
  local copies, waits for them, and re-layouts  0.88 us (1%)
    pallas_call x1, Pallas kernels, fused_per_device(): pl.pallas_call(functools.partial(fused_kernel, n, fn), out_shape=pltpu.VM...  71.7 us

profile of v3, /device:TPU:0, one launch (start us, length us, event | category | flops | bytes accessed | tf_op | source)
XLA Modules:
  0.0 72.6 jit_solution(4184610880705565916)
XLA Ops:
  0.0 71.7 %shard_map.73 = bf16[128,3072]{1,0:T(8,128)(2,1)S(1)} custom-call(bf16[128,3072]{1,0:T(8,128)(2,1)} %bitcast.7, s32[768,3072]{1,0:T(8,128)} %codes.1, f32[6,24]{1,0:T(8,128)} %scales_in.1, bf16[128,3072]{1,0:T(8,128)(2,1)} %bitcast.8, bf16[128,3072]{1,0:T(8,128)(2,1)} %bitcast.9, f32[1,3072]{1,0:T(1,128)} %bitcast.10, f32[1,3072]{1,0:T(1,128)} %bitcast.11), custom_call_target="tpu_custom_call" | custom-call | tf_op jit(solution)/shard_map/pallas_call | solution.py:422
  71.7 0.9 %copy.9 = bf16[1,128,3072]{2,1,0:T(8,128)(2,1)} copy(bf16[1,128,3072]{2,1,0:T(8,128)(2,1)S(1)} %bitcast.6) | data formatting | bytes 1572864

commit v4 on v3

--- a/solution.py
+++ b/solution.py
@@ -127,7 +127,7 @@
 def fused_kernel(
     n, fn, patches, codes, scales_in, key, value, query_gain_in, key_gain_in, out,
     pbuf, cbuf, wbuf, own, kv, qsend, qbuf, obuf, gains, scales,
-    own_sem, code_sem, scale_sem, gain_sem, mate_recv, rest_recv, p_send, first_recv, rest_w_recv, w_send,
+    own_sem, code_sem, scale_sem, gain_sem, mate_recv, partner_recv, rest_recv, p_send, first_recv, rest_w_recv, w_send,
     kv_send, kv_recv, q_send, q_recv, o_send, o_recv, met,
 ):
     s, f = lax.axis_index("seq"), lax.axis_index("fsdp")
@@ -303,7 +303,7 @@
         pl.semaphore_wait(met.at[3], CORES)
 
     start_chip(across(1), 0, 2 * chunks)
-    remote(pbuf.at[rows_of(s)], pbuf.at[rows_of(s)], p_send.at[0], rest_recv.at[0], seq=partner).start()
+    remote(pbuf.at[rows_of(s)], pbuf.at[rows_of(s)], p_send.at[0], partner_recv.at[0], seq=partner).start()
     lax.fori_loop(0, 2 * chunks, start_kv(partner), 0)
 
     def forward():
@@ -311,42 +311,49 @@
         drain(pbuf.at[at], mate_recv.at[0])
         remote(pbuf.at[at], pbuf.at[at], p_send.at[0], rest_recv.at[0], seq=partner).start()
 
+    other = lax.rem(s + m, n)
+    tile = CORES * tokens
+    own_start = pl.multiple_of(place // CORES * tile, tile)
+    beside_start = pl.multiple_of(beside_device // CORES * tile - half * group, tile)
+
+    def project(pair, start, size):
+        at = pl.ds(start, size)
+        there = pl.ds(pl.multiple_of(half * group + start, tile), size)
+        both = jnp.dot(pbuf[at, :], wbuf[pair], preferred_element_type=jnp.float32)
+        for side in range(2):
+            q = 2 * pair + side
+            normed = column_norm(
+                both[:, side * LANES:(side + 1) * LANES], gains[0, :, pl.ds(chunk_column(q), LANES)])
+            if q < chunks:
+                qsend[q, at] = normed
+                remote(qsend.at[q, at], qbuf.at[q, there], q_send.at[0], q_recv.at[q], seq=other).start()
+            else:
+                qbuf[q - chunks, there] = normed
+
+    def weights_in(pair):
+        drain(wbuf.at[pair, pl.ds(0, 2 * rows)], rest_w_recv.at[pair])
+
     relay(0)
     weights_out(1)
+    drain(gains, gain_sem.at[0])
+    drain(pbuf.at[rows_of(s)], partner_recv.at[0])
+    weights_in(0)
+    project(0, own_start, tile)
     pl.when(near)(forward)
     for pair in range(1, chunks - 1):
         relay(pair)
         weights_out(pair + 1)
     pl.when(far)(forward)
-    drain(gains, gain_sem.at[0])
-    drain(pbuf.at[pl.ds(0, chips * tokens)], rest_recv.at[0])
-
-    other = lax.rem(s + m, n)
-    half_rows = pl.ds(pl.multiple_of(half * group, group), group)
-
-    def query_copy(k):
-        return remote(qsend.at[k], qbuf.at[k, half_rows], q_send.at[0], q_recv.at[k], seq=other)
-
-    def project(pair):
-        drain(wbuf.at[pair, pl.ds(0, 2 * rows)], rest_w_recv.at[pair])
-        both = jnp.dot(pbuf[...], wbuf[pair], preferred_element_type=jnp.float32)
-        for side in range(2):
-            q = 2 * pair + side
-            normed = column_norm(
-                both[:, side * LANES:(side + 1) * LANES], gains[0, :, pl.ds(chunk_column(q), LANES)])
-            if q < chunks:
-                qsend[q] = normed
-                query_copy(q).start()
-            else:
-                qbuf[q - chunks, half_rows] = normed
-
-    for pair in range(chunks - 1):
-        project(pair)
+    drain(pbuf.at[rows_of(s)], rest_recv.at[0])
+    project(0, beside_start, tile)
+    for pair in range(1, chunks - 1):
+        weights_in(pair)
+        project(pair, 0, group)
     beside(jnp.where(far, early_units, 0), 2 * chunks)
     relay(chunks - 1)
-    project(chunks - 1)
-
-    tile = CORES * tokens
+    weights_in(chunks - 1)
+    project(chunks - 1, 0, group)
+
     exponent = HDIM ** (-0.5) * math.log2(math.e)
 
     def out_copy(k, to):
@@ -369,7 +376,7 @@
         def _():
             drain(kv.at[k], kv_recv.at[k])
             kv[k, 0] = column_norm(kv[k, 0].astype(jnp.float32), gains[1, :, owned_chunk(s, k)])
-            query_copy(k).wait_recv()
+            drain(qsend.at[k], q_recv.at[k])
 
         values = kv[k, 1]
         keys = kv[k, 0]
@@ -435,7 +442,7 @@
             pltpu.VMEM((chunks, n * tokens, LANES), bf16),
             pltpu.VMEM((2, 1, columns), jnp.float32),
             pltpu.SMEM(block_scales.shape, jnp.float32),
-            dma((2,)), dma((1,)), dma((1,)), dma((1,)), dma((1,)), dma((1,)), dma((1,)),
+            dma((2,)), dma((1,)), dma((1,)), dma((1,)), dma((1,)), dma((1,)), dma((1,)), dma((1,)),
             dma((chunks,)), dma((chunks,)), dma((1,)),
             dma((1,)), dma((chunks,)), dma((1,)), dma((chunks,)), dma((1,)), dma((1,)),
             pltpu.SemaphoreType.REGULAR((4,)),

time: 73.7 us -> 73.4 us (level); the launches traced: 72.6 us -> 73.2 us
  no operation moved by 1% of the time
where the time goes in v4:
time: 73.4 us; the launch traced here: 73.2 us
  Pallas kernels  72.3 us (99%)
  local copies, waits for them, and re-layouts  0.88 us (1%)
    pallas_call x1, Pallas kernels, fused_per_device(): pl.pallas_call(functools.partial(fused_kernel, n, fn), out_shape=pltpu.VM...  72.3 us

profile of v4, /device:TPU:0, one launch (start us, length us, event | category | flops | bytes accessed | tf_op | source)
XLA Modules:
  0.0 73.2 jit_solution(3024642829657489555)
XLA Ops:
  0.0 72.3 %shard_map.73 = bf16[128,3072]{1,0:T(8,128)(2,1)S(1)} custom-call(bf16[128,3072]{1,0:T(8,128)(2,1)} %bitcast.7, s32[768,3072]{1,0:T(8,128)} %codes.1, f32[6,24]{1,0:T(8,128)} %scales_in.1, bf16[128,3072]{1,0:T(8,128)(2,1)} %bitcast.8, bf16[128,3072]{1,0:T(8,128)(2,1)} %bitcast.9, f32[1,3072]{1,0:T(1,128)} %bitcast.10, f32[1,3072]{1,0:T(1,128)} %bitcast.11), custom_call_target="tpu_custom_call" | custom-call | tf_op jit(solution)/shard_map/pallas_call | solution.py:429
  72.3 0.9 %copy.9 = bf16[1,128,3072]{2,1,0:T(8,128)(2,1)} copy(bf16[1,128,3072]{2,1,0:T(8,128)(2,1)S(1)} %bitcast.6) | data formatting | bytes 1572864

commit v5 on v4

--- a/solution.py
+++ b/solution.py
@@ -207,24 +207,21 @@
         return remote(pbuf.at[rows_of(s)], pbuf.at[rows_of(s)], p_send.at[0], mate_recv.at[0], seq=beside_device)
 
     def start_kv(to):
-        def one(unit, _):
-            k, which = unit // 2, lax.rem(unit, 2)
+        def one(k, _):
             remote(
-                own.at[which, :, owned_chunk(to, k)], kv.at[k, which, all_rows_of(s)],
+                own.at[:, :, owned_chunk(to, k)], kv.at[k, :, all_rows_of(s)],
                 kv_send.at[0], kv_recv.at[k], seq=to).start()
             return 0
 
         return one
 
     def start_chip(chip, low, high):
-        def both(unit, _):
+        def both(k, _):
             for c in range(CORES):
-                start_kv(chip * CORES + c)(unit, 0)
+                start_kv(chip * CORES + c)(k, 0)
             return 0
 
         lax.fori_loop(low, high, both, 0)
-
-    early_units = jnp.where(half == 0, 3, 2)
 
     def beside(low, high):
         start_chip(beside_chip, low, high)
@@ -232,7 +229,7 @@
     @pl.when(near)
     def _():
         drain(own, own_sem.at[1])
-        start_chip(across(0), 0, 2 * chunks)
+        start_chip(across(0), 0, chunks)
 
         @pl.when(half == 0)
         def _():
@@ -298,13 +295,13 @@
     def _():
         drain(own, own_sem.at[1])
         pl.semaphore_wait(met.at[0], CORES)
-        start_chip(across(0), 0, 2 * chunks)
-        beside(0, early_units)
+        start_chip(across(0), 0, chunks)
+        beside(0, 1)
         pl.semaphore_wait(met.at[3], CORES)
 
-    start_chip(across(1), 0, 2 * chunks)
+    start_chip(across(1), 0, chunks)
     remote(pbuf.at[rows_of(s)], pbuf.at[rows_of(s)], p_send.at[0], partner_recv.at[0], seq=partner).start()
-    lax.fori_loop(0, 2 * chunks, start_kv(partner), 0)
+    lax.fori_loop(0, chunks, start_kv(partner), 0)
 
     def forward():
         at = rows_of(beside_device)
@@ -349,7 +346,7 @@
     for pair in range(1, chunks - 1):
         weights_in(pair)
         project(pair, 0, group)
-    beside(jnp.where(far, early_units, 0), 2 * chunks)
+    beside(jnp.where(far, 1, 0), chunks)
     relay(chunks - 1)
     weights_in(chunks - 1)
     project(chunks - 1, 0, group)

time: 73.4 us -> 73.5 us (level)
  no operation moved by 1% of the time
where the time goes in v5:
time: 73.5 us; the launch traced here: 73.2 us
  Pallas kernels  72.3 us (98%)
  local copies, waits for them, and re-layouts  0.88 us (1%)
    pallas_call x1, Pallas kernels, fused_per_device(): pl.pallas_call(functools.partial(fused_kernel, n, fn), out_shape=pltpu.VM...  72.3 us

profile of v5, /device:TPU:0, one launch (start us, length us, event | category | flops | bytes accessed | tf_op | source)
XLA Modules:
  0.0 73.2 jit_solution(10751028593114085671)
XLA Ops:
  0.0 72.3 %shard_map.73 = bf16[128,3072]{1,0:T(8,128)(2,1)S(1)} custom-call(bf16[128,3072]{1,0:T(8,128)(2,1)} %bitcast.7, s32[768,3072]{1,0:T(8,128)} %codes.1, f32[6,24]{1,0:T(8,128)} %scales_in.1, bf16[128,3072]{1,0:T(8,128)(2,1)} %bitcast.8, bf16[128,3072]{1,0:T(8,128)(2,1)} %bitcast.9, f32[1,3072]{1,0:T(1,128)} %bitcast.10, f32[1,3072]{1,0:T(1,128)} %bitcast.11), custom_call_target="tpu_custom_call" | custom-call | tf_op jit(solution)/shard_map/pallas_call | solution.py:426
  72.3 0.9 %copy.9 = bf16[1,128,3072]{2,1,0:T(8,128)(2,1)} copy(bf16[1,128,3072]{2,1,0:T(8,128)(2,1)S(1)} %bitcast.6) | data formatting | bytes 1572864

commit v6 on v5

--- a/solution.py
+++ b/solution.py
@@ -391,7 +391,7 @@
             results.append(blended / normaliser)
         obuf[k, here] = jnp.where(first, results[0], results[1]).astype(jnp.bfloat16)
         for c in range(CORES):
-            to = chip * CORES + c
+            to = chip * CORES + lax.rem(core + c, CORES)
 
             @pl.when(to != s)
             def _():

time: 73.5 us -> 73.5 us (level)
  no operation moved by 1% of the time
where the time goes in v6:
time: 73.5 us; the launch traced here: 73.2 us
  Pallas kernels  72.3 us (98%)
  local copies, waits for them, and re-layouts  0.88 us (1%)
    pallas_call x1, Pallas kernels, fused_per_device(): pl.pallas_call(functools.partial(fused_kernel, n, fn), out_shape=pltpu.VM...  72.3 us

profile of v6, /device:TPU:0, one launch (start us, length us, event | category | flops | bytes accessed | tf_op | source)
XLA Modules:
  0.0 73.2 jit_solution(5687228116344945268)
XLA Ops:
  0.0 72.3 %shard_map.73 = bf16[128,3072]{1,0:T(8,128)(2,1)S(1)} custom-call(bf16[128,3072]{1,0:T(8,128)(2,1)} %bitcast.7, s32[768,3072]{1,0:T(8,128)} %codes.1, f32[6,24]{1,0:T(8,128)} %scales_in.1, bf16[128,3072]{1,0:T(8,128)(2,1)} %bitcast.8, bf16[128,3072]{1,0:T(8,128)(2,1)} %bitcast.9, f32[1,3072]{1,0:T(1,128)} %bitcast.10, f32[1,3072]{1,0:T(1,128)} %bitcast.11), custom_call_target="tpu_custom_call" | custom-call | tf_op jit(solution)/shard_map/pallas_call | solution.py:426
  72.3 0.9 %copy.9 = bf16[1,128,3072]{2,1,0:T(8,128)(2,1)} copy(bf16[1,128,3072]{2,1,0:T(8,128)(2,1)S(1)} %bitcast.6) | data formatting | bytes 1572864
